TPU v7x, 32 devices: a whole 2x2x4 slice. The times are simulated.
32 devices in a mesh: blk: 16 (over z, y, core), col: 2 (over x).
Axes of the slice: x: 2, y: 2, z: 4, core: 2. Of those that a mesh axis runs over, the one named last changes fastest.
Arguments:
- encodings: bfloat16 [8192, 1024], P(('blk', 'col')), may hold values from -8 to 8
- first_weight: bfloat16 [1024, 512], replicated, may hold values from -0.1875 to 0.1875
- second_weight: bfloat16 [512, 32], replicated, may hold values from -0.25 to 0.25
- inv_scale: float32 [32], replicated, may hold values from 0.2 to 0.8
- outputscale: float32 [1], replicated, may hold values from 0.5 to 2
- noise: float32 [1], replicated, may hold values from 0.2 to 2
- rhs: float32 [32, 8192], P('col', 'blk'), may hold values from -12 to 12
Outputs:
- solution: float32 [32, 8192], P('col', 'blk')
- residual: float32 [32, 8192], P('col', 'blk')
All inputs are finite; a program needn't handle non-finite values.
Results may differ from a plain program's by a relative error of at most 0.0079.
Values sent between devices are 32-bit elements; how exact they have to be, the bound alone decides.
A program may use at most 64 MiB of HBM per device.

v0:
```python
import jax
import jax.numpy as jnp
from jax import lax
from jax.sharding import PartitionSpec as P


def square_sums(residual):
    return lax.psum(jnp.sum(residual * residual, axis=1), "blk")


def split_blocks(values, width):
    count = values.shape[1] // width
    return values.reshape(values.shape[0], count, width).transpose(1, 0, 2)


def on_device(encodings, first_weight, second_weight, inv_scale, outputscale, noise, rhs):
    hidden = jnp.maximum(
        jnp.dot(encodings, first_weight, preferred_element_type=jnp.float32), 0.0
    ).astype(jnp.bfloat16)
    features = (
        jnp.einsum("hf,nh->fn", second_weight, hidden, preferred_element_type=jnp.float32)
        * inv_scale[:, None]
    )
    paired = lax.all_gather(features, "col", axis=1, tiled=True)
    shard_width = features.shape[1]
    row_norms = jnp.sum(paired * paired, axis=0)
    kernel_scale = outputscale[0]
    nugget = noise[0]
    residual = rhs
    norm_now = square_sums(residual)
    moving = lax.all_to_all(rhs, "col", split_axis=1, concat_axis=0, tiled=True)
    initial = jnp.zeros((moving.shape[0], paired.shape[1]), jnp.float32)

    def advance(running, blocks):
        feat_block, dir_block = blocks
        cross = lax.dot_general(
            paired, feat_block, (((0,), (0,)), ((), ())), precision=lax.Precision.HIGHEST
        )
        distance = (
            row_norms[:, None] + jnp.sum(feat_block * feat_block, axis=0)[None, :] - 2.0 * cross
        )
        kernel_tile = kernel_scale * jnp.exp(-0.5 * distance)
        added = lax.dot_general(
            dir_block, kernel_tile, (((1,), (1,)), ((), ())), precision=lax.Precision.HIGHEST
        )
        return (running + added, None)

    images = lax.scan(
        advance,
        initial,
        (
            split_blocks(lax.all_gather(features, "blk", axis=1, tiled=True), shard_width),
            split_blocks(lax.all_gather(moving, "blk", axis=1, tiled=True), shard_width),
        ),
    )[0]
    images = lax.psum_scatter(images, "col", scatter_dimension=0, tiled=True)
    images = images + nugget * rhs
    bent = lax.psum(jnp.sum(rhs * images, axis=1), "blk")
    step_size = norm_now / bent
    solution = step_size[:, None] * rhs
    residual = residual - step_size[:, None] * images
    return (solution, residual)


def solution(mesh):
    placed = (P(("blk", "col"), None), P(), P(), P(), P(), P(), P("col", "blk"))
    return jax.shard_map(
        on_device,
        mesh=mesh,
        in_specs=placed,
        out_specs=(P("col", "blk"), P("col", "blk")),
        check_vma=False,
    )
```

profile of v0, /device:TPU:0, one launch (start us, length us, event | category | flops | bytes accessed | tf_op | source)
XLA Modules:
  0.0 143.1 jit_solution(18136698835859300657)
XLA Ops:
  7.2 1.5 %copy.27 = f32[2,2,8,256]{3,2,0,1:T(8,128)} copy(f32[2,2,8,256]{3,2,1,0:T(8,128)} %bitcast.64) | data formatting | bytes 65536 | tf_op jit(solution)/shard_map/all_to_all | solution.py:31
  8.6 4.4 %all-to-all-start = ((f32[16,2,256]{2,0,1:T(8,128)}), f32[16,2,256]{2,0,1:T(8,128)S(1)}, u32[]{:S(2)}, u32[]{:S(2)}) async-start(f32[16,2,256]{2,0,1:T(8,128)} %bitcast.45), calls=%async_computation | async-start | bytes 65536 | tf_op jit(solution)/shard_map/all_to_all | solution.py:31
  13.0 1.6 %fusion.12 = f32[32,256]{1,0:T(8,128)S(1)} fusion(bf16[512,32]{0,1:T(8,128)(2,1)S(1)} %copy-done.4, bf16[256,1024]{1,0:T(8,128)(2,1)} %param.9, bf16[1024,512]{1,0:T(8,128)(2,1)S(1)} %copy-done, f32[32]{0:T(128)S(1)} %copy-done.5), kind=kOutput, calls=%fused_computation.18 | convolution fusion | flops 277094400 | bytes 1638528 | tf_op jit(solution)/shard_map/hf,nh->fn/dot_general | solution.py:21
  14.6 4.6 %all_gather.10 = f32[32,512]{1,0:T(8,128)S(1)} all-gather(f32[32,256]{1,0:T(8,128)S(1)} %fusion.12), channel_id=1, replica_groups=mesh['blk'=16,'col'=2] {'col'}, dimensions={1}, use_global_device_ids=true | all-gather | bytes 98304 | tf_op jit(solution)/shard_map/all_gather | solution.py:24
  19.2 23.8 %all_gather.11 = f32[32,4096]{1,0:T(8,128)S(1)} all-gather(f32[32,256]{1,0:T(8,128)S(1)} %fusion.12), channel_id=1, replica_groups=mesh['blk'=16,'col'=2] {'blk'}, dimensions={1}, use_global_device_ids=true | all-gather | bytes 557056 | tf_op jit(solution)/shard_map/all_gather | solution.py:52
  43.1 18.9 %all_gather.9 = f32[32,4096]{1,0:T(8,128)S(1)} all-gather(f32[32,256]{1,0:T(8,128)S(1)} %bitcast.65), channel_id=1, replica_groups=mesh['blk'=16,'col'=2] {'blk'}, dimensions={1}, use_global_device_ids=true | all-gather | bytes 557056 | tf_op jit(solution)/shard_map/all_gather | solution.py:53
  62.2 30.2 %while.11 = (s32[]{:T(128)}, f32[32,512]{1,0:T(8,128)S(1)}, f32[16,32,256]{2,0,1:T(8,128)S(1)}, f32[]{:T(128)}, f32[512]{0:T(512)S(1)}, /*index=5*/f32[16,32,256...) while((s32[]{:T(128)}, f32[32,512]{1,0:T(8,128)S(1)}, f32[16,32,256]{2,0,1:T(8,128)S(1)}, ...), condition=%wide.region_5.6_spmd.clone, body=%wide.region_3.5_spmd.clone.sunk | while | flops 101367552 | bytes 1413239 | solution.py:48
  64.1 1.4 fusion.29
  66.0 1.4 fusion.29
  67.9 1.4 fusion.29
  69.7 1.4 fusion.29
  71.6 1.4 fusion.29
  73.5 1.4 fusion.29
  75.4 1.4 fusion.29
  77.3 1.4 fusion.29
  79.2 1.4 fusion.29
  81.1 1.4 fusion.29
  82.9 1.4 fusion.29
  84.8 1.4 fusion.29
  86.7 1.4 fusion.29
  88.6 1.4 fusion.29
  90.5 1.4 fusion.29
  93.6 8.3 %reduce-scatter.2.cloned.1.call-done = f32[16,512]{1,0:T(8,128)} async-done(((f32[32,512]{1,0:T(8,128)}), f32[16,512]{1,0:T(8,128)}) %reduce-scatter.2.cloned.1.call-update) | async-done | bytes 32784 | tf_op jit(solution)/shard_map/reduce_scatter | solution.py:56
  102.9 32.6 %all-reduce = (f32[16]{0:T(128)S(1)}, f32[16]{0:T(128)S(1)}) all-reduce(f32[16]{0:T(128)S(1)} %get-tuple-element.86, f32[16]{0:T(128)S(1)} %get-tuple-element.85), channel_id=1, replica_groups=mesh['blk'=16,'col'=2] {'blk'}, use_global_device_ids=true, to_apply=%region_1.0 | all-reduce | flops 32 | bytes 256 | tf_op jit(solution)/shard_map/psum | solution.py:8
  (71 shorter events, 11.5 us)
Async XLA Ops:
  7.2 5.9 %copy-start = (bf16[1024,512]{1,0:T(8,128)(2,1)S(1)}, bf16[1024,512]{1,0:T(8,128)(2,1)}, u32[]{:S(2)}) copy-start(bf16[1024,512]{1,0:T(8,128)(2,1)} %param.10) | copy-start | bytes 3145732
  8.6 4.4 %copy-start.4 = (bf16[512,32]{0,1:T(8,128)(2,1)S(1)}, bf16[512,32]{0,1:T(8,128)(2,1)}, u32[]{:S(2)}) copy-start(bf16[512,32]{0,1:T(8,128)(2,1)} %param.11) | copy-start | bytes 98308
  8.6 4.4 %copy-start.5 = (f32[32]{0:T(128)S(1)}, f32[32]{0:T(128)}, u32[]{:S(2)}) copy-start(f32[32]{0:T(128)} %param.12) | copy-start | bytes 388
  8.6 34.5 %all-to-all-start = ((f32[16,2,256]{2,0,1:T(8,128)}), f32[16,2,256]{2,0,1:T(8,128)S(1)}, u32[]{:S(2)}, u32[]{:S(2)}) async-start(f32[16,2,256]{2,0,1:T(8,128)} %bitcast.45), calls=%async_computation | async-start | bytes 65536 | tf_op jit(solution)/shard_map/all_to_all | solution.py:31
  13.0 89.0 %reduce-scatter.2.cloned.1.call-start = ((), (), s32[]{:S(2)}) async-start(), calls=%async_computation.2 | async-start | bytes 98304 | tf_op jit(solution)/shard_map/reduce_scatter | solution.py:56
  92.3 0.6 copy-start.1
  92.3 9.6 %copy-start.2 = (f32[16,512]{1,0:T(8,128)S(1)}, f32[16,512]{1,0:T(8,128)}, u32[]{:S(2)}) copy-start(f32[16,512]{1,0:T(8,128)} %param.15) | copy-start | bytes 98308
  102.0 33.6 %copy-start.3 = (f32[16,512]{1,0:T(8,128)S(1)}, f32[16,512]{1,0:T(8,128)}, u32[]{:S(2)}) copy-start(f32[16,512]{1,0:T(8,128)} %reduce-scatter.2.cloned.1.call-done) | copy-start | bytes 98308
Sparse Core Ops, SparseCore 0:
  93.1 8.8 reduce-scatter.1
where the time goes:
time: 144 us; the launch traced here: 143 us
  blocking collectives  79.8 us (55%)
  matrix products  30.1 us (21%)
  between operations  14.7 us (10%)
  waiting for transfers between devices  8.35 us (6%)
  starting transfers between devices  4.37 us (3%)
  local copies, waits for them, and re-layouts  2.89 us (2%)
  other arithmetic  2.1 us (1%)
    psum x1, blocking collectives, square_sums(): return lax.psum(jnp.sum(residual * residual, axis=1), 'blk')  32.6 us
    all_gather x1, blocking collectives, on_device(): lax.all_gather(features, 'blk', axis=1, tiled=True)  23.8 us
    dot_general x16, matrix products, advance(): lax.dot_general(paired, feat_block, (((0,), (0,)), ((), ())), precision=l...  21.9 us
    all_gather x1, blocking collectives, on_device(): lax.all_gather(moving, 'blk', axis=1, tiled=True)  18.9 us
    reduce_scatter x1, waiting for transfers between devices, on_device(): images = lax.psum_scatter(images, 'col', scatter_dimension=0, tiled=True)  8.33 us
    dot_general x16, matrix products, advance(): lax.dot_general(dir_block, kernel_tile, (((1,), (1,)), ((), ())), precisi...  6.59 us
    all_gather x1, blocking collectives, on_device(): paired = lax.all_gather(features, 'col', axis=1, tiled=True)  4.59 us
    all_to_all x1, starting transfers between devices, on_device(): moving = lax.all_to_all(rhs, 'col', split_axis=1, concat_axis=0, tiled=True)  4.37 us
  transfers between devices with their start and end apart: 2, of which 1 were waited for; matrix products, arithmetic and copies ran while one was open for 1% of the time, Pallas kernels for 0%

commit v1 on v0

v1 whole, which is shorter than its diff:
```python
import functools
import math

import jax
import jax.numpy as jnp
from jax import lax
from jax.experimental import pallas as pl
from jax.experimental.pallas import tpu as pltpu
from jax.sharding import PartitionSpec as P

MESH = pl.DeviceIdType.MESH
F32 = jnp.float32
BF16 = jnp.bfloat16
ROOT_LOG2E = math.sqrt(math.log2(math.e))


def split3(values):
    high = values.astype(BF16)
    rest = values - high.astype(F32)
    mid = rest.astype(BF16)
    low = (rest - mid.astype(F32)).astype(BF16)
    return high, mid, low


def stacked(points, mine):
    width = points.shape[1]
    points = points * ROOT_LOG2E
    high, mid, low = split3(points)
    half_norm = -0.5 * jnp.sum(points * points, axis=0, keepdims=True)
    parts = [part.astype(F32) for part in split3(half_norm)]
    row = lax.broadcasted_iota(jnp.int32, (16, width), 0)
    first = 3 if mine else 0
    extra = jnp.where(row < 6, 1.0, 0.0).astype(F32)
    for at, part in enumerate(parts):
        extra = jnp.where(row == first + at, part, extra)
    extra = extra.astype(BF16)
    order = [high, high, mid, high, low, mid] if mine else [high, mid, high, low, high, mid]
    used = 6 * points.shape[0] + 16
    total = -(-used // 256) * 256
    return jnp.concatenate(order + [extra, jnp.zeros((total - used, width), BF16)], axis=0)


def kernel(
    nblk, ncol,
    enc_hbm, w1_hbm, w2_ref, inv_ref, scale_ref, noise_ref, rhs_hbm,
    sol_ref, res_ref,
    enc, w1, xall, vall, mine_t, acc, bent,
    load_sem, x_recv, v_recv, b_recv,
    x_out_s, x_mid_s, x_col_s, x_core_s, v_out_s, v_mid_s, v_core_s, b_send,
):
    no = nblk // 4
    blk = lax.axis_index("blk")
    col = lax.axis_index("col")
    out, mid, core = blk // 4, (blk // 2) % 2, blk % 2
    width = xall.shape[2]
    steps = ncol * 2 * no

    def blk_of(o, m, c):
        return (o * 2 + m) * 2 + c

    mid_peer = (blk_of(out, 1 - mid, core), col)
    core_peer = (blk_of(out, mid, 1 - core), col)

    barrier = pltpu.get_barrier_semaphore()
    for d in range(1, nblk):
        pl.semaphore_signal(barrier, inc=1, device_id=(lax.rem(blk + d, nblk), col), device_id_type=MESH)
    for d in range(1, ncol):
        pl.semaphore_signal(barrier, inc=1, device_id=(blk, lax.rem(col + d, ncol)), device_id_type=MESH)

    rhs_load = pltpu.make_async_copy(rhs_hbm, vall.at[blk], load_sem.at[0])
    w1_load = pltpu.make_async_copy(w1_hbm, w1, load_sem.at[1])
    enc_load = pltpu.make_async_copy(enc_hbm, enc, load_sem.at[2])
    rhs_load.start()
    enc_load.start()
    w1_load.start()

    def send(ref, at, peer, send_sem, recv_sem):
        return pltpu.make_async_remote_copy(
            src_ref=ref.at[at], dst_ref=ref.at[at], send_sem=send_sem, recv_sem=recv_sem,
            device_id=peer, device_id_type=MESH,
        )

    def x_send(g, peer, sem):
        return send(xall, g, peer, sem, x_recv.at[g])

    def v_send(b, peer, sem):
        return send(vall, b, peer, sem, v_recv.at[b])

    def col_peer(d):
        return (blk, lax.rem(col + d, ncol))

    def out_peer(d):
        return (blk_of(lax.rem(out + d, no), mid, core), col)

    rhs_load.wait()
    pl.semaphore_wait(barrier, nblk - 1 + ncol - 1)
    for d in range(1, no):
        v_send(blk, out_peer(d), v_out_s.at[d]).start()
    v_send(blk, mid_peer, v_mid_s.at[0]).start()
    v_send(blk, core_peer, v_core_s.at[0]).start()

    enc_load.wait()
    w1_load.wait()
    hidden = jnp.maximum(jnp.dot(enc[...], w1[...], preferred_element_type=F32), 0.0).astype(BF16)
    features = jnp.dot(hidden, w2_ref[...], preferred_element_type=F32) * inv_ref[...]
    me = blk * ncol + col
    xall[me] = features.T
    acc[...] = jnp.zeros_like(acc)

    for d in range(1, no):
        x_send(me, out_peer(d), x_out_s.at[d]).start()
    x_send(me, mid_peer, x_mid_s.at[0]).start()
    for d in range(1, ncol):
        x_send(me, col_peer(d), x_col_s.at[d - 1, 0]).start()
    x_send(me, core_peer, x_core_s.at[0]).start()

    for d in range(1, no):
        b = blk_of(lax.rem(out + d, no), mid, core)
        v_send(b, mid_peer, v_mid_s.at[d]).wait_recv()
        v_send(b, mid_peer, v_mid_s.at[d]).start()
        v_send(b, core_peer, v_core_s.at[d]).start()

    for d in range(1, ncol):
        g = blk * ncol + lax.rem(col + d, ncol)
        x_send(g, core_peer, x_core_s.at[0]).wait_recv()
    for k in range(ncol):
        rows = stacked(xall[blk * ncol + k], True)
        mine_t[pl.ds(k * width, width), :] = rows.T

    def place(s):
        dk, dm, do = s // (2 * no), (s // no) % 2, s % no
        o, m, k = lax.rem(out + do, no), lax.rem(mid + dm, 2), lax.rem(col + dk, ncol)
        return dk, dm, do, o, m, k

    def product(b, k):
        rows = stacked(xall[b * ncol + k], False)
        vec = jnp.concatenate(split3(vall[b, :, pl.ds(pl.multiple_of(k * width, width), width)]), axis=0)
        logs = jnp.dot(mine_t[...], rows, preferred_element_type=F32)
        tile = jnp.exp2(logs).astype(BF16)
        return lax.dot_general(tile, vec, (((1,), (1,)), ((), ())), preferred_element_type=F32)

    def step(s, carry):
        dk, dm, do, o, m, k = place(s)
        b = blk_of(o, m, core)
        g = b * ncol + k

        @pl.when(jnp.logical_and(s < steps, s > 0))
        def _():
            @pl.when(jnp.logical_or(dk == 0, s % (2 * no) > 0))
            def _():
                x_send(g, core_peer, x_core_s.at[s]).wait_recv()

            x_send(g, core_peer, x_core_s.at[s]).start()

            @pl.when(dk == 0)
            def _():
                for d in range(1, ncol):
                    x_send(g, col_peer(d), x_col_s.at[d - 1, s]).start()

                @pl.when(dm == 0)
                def _():
                    x_send(g, mid_peer, x_mid_s.at[s]).start()

                @pl.when(dm == 1)
                def _():
                    v_send(b, core_peer, v_core_s.at[s]).wait_recv()
                    v_send(b, core_peer, v_core_s.at[s]).start()

        @pl.when(s >= 2)
        def _():
            dk, dm, do, o, m, k = place(s - 2)
            other = blk_of(o, m, 1 - core)
            x_send(other * ncol + k, core_peer, x_core_s.at[s - 2]).wait_recv()

            @pl.when(dk == 0)
            def _():
                v_send(other, core_peer, v_core_s.at[s - 2]).wait_recv()

            acc[...] += product(blk_of(o, m, core), k) + product(other, k)

        return carry

    lax.fori_loop(0, steps + 2, step, 0)

    rhs = vall[blk]
    count = rhs.shape[0]
    acc_t = acc[...].T
    image = acc_t[:count] + acc_t[count : 2 * count] + acc_t[2 * count :]
    image = scale_ref[0] * image + noise_ref[0] * rhs
    bent[blk] = jnp.broadcast_to(jnp.sum(rhs * image, axis=1, keepdims=True), bent.shape[1:])

    total = jnp.zeros_like(rhs)
    total = lax.fori_loop(0, nblk, lambda b, t: t + vall[b] * vall[b], total)
    norm = jnp.sum(total, axis=1, keepdims=True)

    def bent_send(d, b):
        return send(bent, b, (lax.rem(blk + d, nblk), col), b_send.at[d], b_recv.at[b])

    for d in range(1, nblk):
        bent_send(d, blk).start()
    for d in range(1, nblk):
        bent_send(d, lax.rem(blk + d, nblk)).wait_recv()
    curve = jnp.sum(bent[...], axis=0)[:, :1]
    alpha = norm / curve
    sol_ref[...] = alpha * rhs
    res_ref[...] = rhs - alpha * image

    for d in range(1, nblk):
        bent_send(d, blk).wait_send()
    for d in range(1, no):
        v_send(blk, out_peer(d), v_out_s.at[d]).wait_send()
        x_send(me, out_peer(d), x_out_s.at[d]).wait_send()

    def settle(s, carry):
        x_send(me, core_peer, x_core_s.at[s]).wait_send()

        @pl.when(s < 2 * no)
        def _():
            v_send(blk, core_peer, v_core_s.at[s]).wait_send()
            for d in range(1, ncol):
                x_send(me, core_peer, x_col_s.at[d - 1, s]).wait_send()

        @pl.when(s < no)
        def _():
            x_send(me, core_peer, x_mid_s.at[s]).wait_send()
            v_send(blk, core_peer, v_mid_s.at[s]).wait_send()

        return carry

    lax.fori_loop(0, steps, settle, 0)


def solution(mesh):
    nblk, ncol = mesh.shape["blk"], mesh.shape["col"]
    no = nblk // 4

    def on_device(encodings, first_weight, second_weight, inv_scale, outputscale, noise, rhs):
        half, feat = encodings.shape[0], second_weight.shape[1]
        cols, points = rhs.shape
        depth = -(-(6 * feat + 16) // 256) * 256
        dma = pltpu.SemaphoreType.DMA
        vmem = pl.BlockSpec(memory_space=pltpu.VMEM)
        smem = pl.BlockSpec(memory_space=pltpu.SMEM)
        hbm = pl.BlockSpec(memory_space=pl.ANY)
        out = jax.ShapeDtypeStruct(rhs.shape, F32)
        return pl.pallas_call(
            functools.partial(kernel, nblk, ncol),
            out_shape=(out, out),
            in_specs=[hbm, hbm, vmem, vmem, smem, smem, hbm],
            out_specs=(vmem, vmem),
            scratch_shapes=[
                pltpu.VMEM(encodings.shape, BF16),
                pltpu.VMEM(first_weight.shape, BF16),
                pltpu.VMEM((nblk * ncol, feat, half), F32),
                pltpu.VMEM((nblk, cols, points), F32),
                pltpu.VMEM((points, depth), BF16),
                pltpu.VMEM((points, 3 * cols), F32),
                pltpu.VMEM((nblk, cols, 128), F32),
                dma((3,)),
                dma((nblk * ncol,)),
                dma((nblk,)),
                dma((nblk,)),
                dma((no,)),
                dma((no,)),
                dma((max(ncol - 1, 1), 2 * no)),
                dma((2 * no * ncol,)),
                dma((no,)),
                dma((no,)),
                dma((2 * no,)),
                dma((nblk,)),
            ],
            compiler_params=pltpu.CompilerParams(collective_id=0, has_side_effects=True),
        )(encodings, first_weight, second_weight, inv_scale.reshape(1, feat), outputscale, noise, rhs)

    placed = (P(("blk", "col"), None), P(), P(), P(), P(), P(), P("col", "blk"))
    return jax.shard_map(
        on_device,
        mesh=mesh,
        in_specs=placed,
        out_specs=(P("col", "blk"), P("col", "blk")),
        check_vma=False,
    )
```

time: 144 us -> 36.2 us (0.25)
  blocking collectives: 79.8 us -> 0 us
  Pallas kernels: 0 us -> 30.5 us
  matrix products: 30.1 us -> 0 us
  between operations: 14.7 us -> 1.94 us
  waiting for transfers between devices: 8.35 us -> 0 us
  starting transfers between devices: 4.37 us -> 0 us
  other arithmetic: 2.1 us -> 0 us
    all_gather x3 -> x0, blocking collectives: 47.2 us -> none  [the longest x1 23.8 us: on_device(): lax.all_gather(features, 'blk', axis=1, tiled=True)]
    psum x1 -> x0, blocking collectives: 32.6 us -> none  [square_sums(): return lax.psum(jnp.sum(residual * residual, axis=1), 'blk')]
    pallas_call x0 -> x1, Pallas kernels: none -> 30.5 us  [on_device(): pl.pallas_call(functools.partial(kernel, nblk, ncol), out_shape=(out, out...]
    dot_general x33 -> x0, matrix products: 30.1 us -> none  [the longest x16 21.9 us: advance(): lax.dot_general(paired, feat_block, (((0,), (0,)), ((), ())), precision=l...]
    reduce_scatter x1 -> x0, waiting for transfers between devices: 8.33 us -> none  [on_device(): images = lax.psum_scatter(images, 'col', scatter_dimension=0, tiled=True)]
    all_to_all x1 -> x0, starting transfers between devices: 4.37 us -> none  [on_device(): moving = lax.all_to_all(rhs, 'col', split_axis=1, concat_axis=0, tiled=True)]
    unnamed x13 -> x5, local copies, waits for them, and re-layouts: 0.79 us -> 3.5 us
    all_to_all x1 -> x0, local copies, waits for them, and re-layouts: 1.46 us -> none  [on_device(): moving = lax.all_to_all(rhs, 'col', split_axis=1, concat_axis=0, tiled=True)]
  transfers between devices with their start and end apart: 2 -> 0, of which waited for: 1 -> 0; matrix products, arithmetic and copies ran while one was open for 1% -> 0% of each run, Pallas kernels for 0% -> 0%
where the time goes in v1:
time: 36.2 us; the launch traced here: 35.9 us
  Pallas kernels  30.5 us (84%)
  local copies, waits for them, and re-layouts  3.5 us (10%)
  between operations  1.94 us (5%)
    pallas_call x1, Pallas kernels, on_device(): pl.pallas_call(functools.partial(kernel, nblk, ncol), out_shape=(out, out...  30.5 us
    unnamed x5, local copies, waits for them, and re-layouts  3.5 us

profile of v1, /device:TPU:0, one launch (start us, length us, event | category | flops | bytes accessed | tf_op | source)
XLA Modules:
  0.0 35.9 jit_solution(8921787252418826840)
XLA Ops:
  1.9 1.5 %copy.9.w2_ref = bf16[512,32]{1,0:T(8,128)(2,1)} copy(bf16[512,32]{0,1:T(8,128)(2,1)} %param.9) | data formatting | bytes 65536 | tf_op args[2]
  3.4 30.5 %shard_map.86 = (f32[16,512]{1,0:T(8,128)}, f32[16,512]{1,0:T(8,128)}) custom-call(bf16[256,1024]{1,0:T(8,128)(2,1)} %enc_hbm.1, bf16[1024,512]{1,0:T(8,128)(2,1)} %w1_hbm.1, bf16[512,32]{1,0:T(8,128)(2,1)} %copy.9.w2_ref, f32[1,32]{1,0:T(1,128)} %bitcast.1, f32[1]{0:T(128)S(6)} %copy.12.scale_ref, f32[1]{0:T(128)S(6)} %copy.13.noise_ref, f32[16,512]{1,0:T(8,128)} %rhs_hbm.1), custom_call_target="tpu_custom_call" | custom-call | tf_op jit(solution)/shard_map/pallas_call | solution.py:246
  33.9 0.0 copy-start
  33.9 1.4 %copy.14 = f32[16,512]{1,0:T(8,128)} copy(f32[16,512]{1,0:T(8,128)} %get-tuple-element.4) | data formatting | bytes 65536
  35.3 0.0 copy-done
  35.3 0.6 %copy.15 = f32[16,512]{1,0:T(8,128)} copy(f32[16,512]{1,0:T(8,128)S(1)} %copy-done) | data formatting | bytes 65536
Async XLA Ops:
  33.9 1.4 %copy-start = (f32[16,512]{1,0:T(8,128)S(1)}, f32[16,512]{1,0:T(8,128)}, u32[]{:S(2)}) copy-start(f32[16,512]{1,0:T(8,128)} %get-tuple-element.5) | copy-start | bytes 98308

commit v2 on v1

--- a/solution.py
+++ b/solution.py
@@ -40,11 +40,23 @@
     return jnp.concatenate(order + [extra, jnp.zeros((total - used, width), BF16)], axis=0)
 
 
+def to_column(row, count):
+    shape = (count, row.shape[1])
+    same = lax.broadcasted_iota(jnp.int32, shape, 0) == lax.broadcasted_iota(jnp.int32, shape, 1)
+    return jnp.sum(jnp.where(same, row, 0.0), axis=1, keepdims=True)
+
+
+def to_row(column, width):
+    shape = (column.shape[0], width)
+    same = lax.broadcasted_iota(jnp.int32, shape, 0) == lax.broadcasted_iota(jnp.int32, shape, 1)
+    return jnp.sum(jnp.where(same, column, 0.0), axis=0, keepdims=True)
+
+
 def kernel(
     nblk, ncol,
-    enc_hbm, w1_hbm, w2_ref, inv_ref, scale_ref, noise_ref, rhs_hbm,
-    sol_ref, res_ref,
-    enc, w1, xall, vall, mine_t, acc, bent,
+    enc_hbm, w1_hbm, w2_hbm, inv_hbm, scale_hbm, noise_hbm, rhs_hbm,
+    alpha_ref, image_ref,
+    enc, w1, w2_ref, inv_ref, scale_ref, noise_ref, xall, vall, mine_t, acc, bent,
     load_sem, x_recv, v_recv, b_recv,
     x_out_s, x_mid_s, x_col_s, x_core_s, v_out_s, v_mid_s, v_core_s, b_send,
 ):
@@ -70,9 +82,17 @@
     rhs_load = pltpu.make_async_copy(rhs_hbm, vall.at[blk], load_sem.at[0])
     w1_load = pltpu.make_async_copy(w1_hbm, w1, load_sem.at[1])
     enc_load = pltpu.make_async_copy(enc_hbm, enc, load_sem.at[2])
+    small_loads = [
+        pltpu.make_async_copy(source, target, load_sem.at[3 + at])
+        for at, (source, target) in enumerate(
+            ((w2_hbm, w2_ref), (inv_hbm, inv_ref), (scale_hbm, scale_ref), (noise_hbm, noise_ref))
+        )
+    ]
     rhs_load.start()
     enc_load.start()
     w1_load.start()
+    for load in small_loads:
+        load.start()
 
     def send(ref, at, peer, send_sem, recv_sem):
         return pltpu.make_async_remote_copy(
@@ -99,12 +119,14 @@
     v_send(blk, mid_peer, v_mid_s.at[0]).start()
     v_send(blk, core_peer, v_core_s.at[0]).start()
 
+    for load in small_loads:
+        load.wait()
     enc_load.wait()
     w1_load.wait()
     hidden = jnp.maximum(jnp.dot(enc[...], w1[...], preferred_element_type=F32), 0.0).astype(BF16)
-    features = jnp.dot(hidden, w2_ref[...], preferred_element_type=F32) * inv_ref[...]
+    features = lax.dot_general(w2_ref[...], hidden, (((1,), (1,)), ((), ())), preferred_element_type=F32)
     me = blk * ncol + col
-    xall[me] = features.T
+    xall[me] = features * to_column(inv_ref[...], features.shape[0])
     acc[...] = jnp.zeros_like(acc)
 
     for d in range(1, no):
@@ -186,8 +208,9 @@
     count = rhs.shape[0]
     acc_t = acc[...].T
     image = acc_t[:count] + acc_t[count : 2 * count] + acc_t[2 * count :]
-    image = scale_ref[0] * image + noise_ref[0] * rhs
-    bent[blk] = jnp.broadcast_to(jnp.sum(rhs * image, axis=1, keepdims=True), bent.shape[1:])
+    image = scale_ref[...] * image + noise_ref[...] * rhs
+    image_ref[...] = image
+    bent[blk] = to_row(jnp.sum(rhs * image, axis=1, keepdims=True), bent.shape[2])
 
     total = jnp.zeros_like(rhs)
     total = lax.fori_loop(0, nblk, lambda b, t: t + vall[b] * vall[b], total)
@@ -200,10 +223,8 @@
         bent_send(d, blk).start()
     for d in range(1, nblk):
         bent_send(d, lax.rem(blk + d, nblk)).wait_recv()
-    curve = jnp.sum(bent[...], axis=0)[:, :1]
-    alpha = norm / curve
-    sol_ref[...] = alpha * rhs
-    res_ref[...] = rhs - alpha * image
+    curve = to_column(jnp.sum(bent[...], axis=0), count)
+    alpha_ref[...] = jnp.broadcast_to(norm / curve, rhs.shape)
 
     for d in range(1, nblk):
         bent_send(d, blk).wait_send()
@@ -240,23 +261,26 @@
         depth = -(-(6 * feat + 16) // 256) * 256
         dma = pltpu.SemaphoreType.DMA
         vmem = pl.BlockSpec(memory_space=pltpu.VMEM)
-        smem = pl.BlockSpec(memory_space=pltpu.SMEM)
         hbm = pl.BlockSpec(memory_space=pl.ANY)
         out = jax.ShapeDtypeStruct(rhs.shape, F32)
-        return pl.pallas_call(
+        alpha, image = pl.pallas_call(
             functools.partial(kernel, nblk, ncol),
             out_shape=(out, out),
-            in_specs=[hbm, hbm, vmem, vmem, smem, smem, hbm],
+            in_specs=[hbm] * 7,
             out_specs=(vmem, vmem),
             scratch_shapes=[
                 pltpu.VMEM(encodings.shape, BF16),
                 pltpu.VMEM(first_weight.shape, BF16),
+                pltpu.VMEM((feat, second_weight.shape[0]), BF16),
+                pltpu.VMEM((1, feat), F32),
+                pltpu.VMEM((1, 1), F32),
+                pltpu.VMEM((1, 1), F32),
                 pltpu.VMEM((nblk * ncol, feat, half), F32),
                 pltpu.VMEM((nblk, cols, points), F32),
                 pltpu.VMEM((points, depth), BF16),
                 pltpu.VMEM((points, 3 * cols), F32),
-                pltpu.VMEM((nblk, cols, 128), F32),
-                dma((3,)),
+                pltpu.VMEM((nblk, 1, 128), F32),
+                dma((7,)),
                 dma((nblk * ncol,)),
                 dma((nblk,)),
                 dma((nblk,)),
@@ -270,7 +294,9 @@
                 dma((nblk,)),
             ],
             compiler_params=pltpu.CompilerParams(collective_id=0, has_side_effects=True),
-        )(encodings, first_weight, second_weight, inv_scale.reshape(1, feat), outputscale, noise, rhs)
+        )(encodings, first_weight, second_weight.T, inv_scale.reshape(1, feat),
+          outputscale.reshape(1, 1), noise.reshape(1, 1), rhs)
+        return alpha * rhs, rhs - alpha * image
 
     placed = (P(("blk", "col"), None), P(), P(), P(), P(), P(), P("col", "blk"))
     return jax.shard_map(

time: 36.2 us -> 33.1 us (0.914)
  local copies, waits for them, and re-layouts: 3.5 us -> 0.01 us
  other arithmetic: 0 us -> 1.41 us
  Pallas kernels: 30.5 us -> 29.5 us
    unnamed x5 -> x2, local copies, waits for them, and re-layouts: 3.5 us -> 0.01 us
    sub x0 -> x1, other arithmetic: none -> 1.41 us  [on_device(): return (alpha * rhs, rhs - alpha * image)]
    pallas_call x1, Pallas kernels: 30.5 us -> 29.5 us  [on_device(): pl.pallas_call(functools.partial(kernel, nblk, ncol), out_shape=(out, out...]
where the time goes in v2:
time: 33.1 us; the launch traced here: 32.9 us
  Pallas kernels  29.5 us (89%)
  between operations  1.95 us (6%)
  other arithmetic  1.41 us (4%)
    pallas_call x1, Pallas kernels, on_device(): pl.pallas_call(functools.partial(kernel, nblk, ncol), out_shape=(out, out...  29.5 us
    sub x1, other arithmetic, on_device(): return (alpha * rhs, rhs - alpha * image)  1.41 us

profile of v2, /device:TPU:0, one launch (start us, length us, event | category | flops | bytes accessed | tf_op | source)
XLA Modules:
  0.0 32.9 jit_solution(14386570031005190171)
XLA Ops:
  1.9 0.0 copy-start
  1.9 29.5 %shard_map.86 = (f32[16,512]{1,0:T(8,128)}, f32[16,512]{1,0:T(8,128)}) custom-call(bf16[256,1024]{1,0:T(8,128)(2,1)} %enc_hbm.1, bf16[1024,512]{1,0:T(8,128)(2,1)} %w1_hbm.1, bf16[32,512]{1,0:T(8,128)(2,1)} %bitcast.6, f32[1,32]{1,0:T(1,128)} %bitcast.7, f32[1,1]{1,0:T(1,128)} %bitcast.4.scale_hbm, f32[1,1]{1,0:T(1,128)} %bitcast.5.noise_hbm, f32[16,512]{1,0:T(8,128)} %rhs_hbm.1), custom_call_target="tpu_custom_call" | custom-call | tf_op jit(solution)/shard_map/pallas_call | solution.py:266
  31.5 0.0 copy-done
  31.5 1.4 %multiply_subtract_fusion = (f32[16,512]{1,0:T(8,128)}, f32[16,512]{1,0:T(8,128)}) fusion(f32[16,512]{1,0:T(8,128)S(1)} %copy-done, f32[16,512]{1,0:T(8,128)} %get-tuple-element.4, f32[16,512]{1,0:T(8,128)} %get-tuple-element.5), kind=kLoop, calls=%fused_computation | loop fusion | flops 24576 | bytes 163840 | tf_op jit(solution)/shard_map/sub | solution.py:299
Async XLA Ops:
  1.9 29.5 %copy-start = (f32[16,512]{1,0:T(8,128)S(1)}, f32[16,512]{1,0:T(8,128)}, u32[]{:S(2)}) copy-start(f32[16,512]{1,0:T(8,128)} %rhs_hbm.1) | copy-start | bytes 98308

commit v3 on v2

v3 whole, which is shorter than its diff:
```python
import functools
import math

import jax
import jax.numpy as jnp
from jax import lax
from jax.experimental import pallas as pl
from jax.experimental.pallas import tpu as pltpu
from jax.sharding import PartitionSpec as P

MESH = pl.DeviceIdType.MESH
F32 = jnp.float32
BF16 = jnp.bfloat16
ROOT_LOG2E = math.sqrt(math.log2(math.e))


def split3(values):
    high = values.astype(BF16)
    rest = values - high.astype(F32)
    mid = rest.astype(BF16)
    low = (rest - mid.astype(F32)).astype(BF16)
    return high, mid, low


def stacked(points, mine):
    width = points.shape[1]
    points = points * ROOT_LOG2E
    high, mid, low = split3(points)
    half_norm = -0.5 * jnp.sum(points * points, axis=0, keepdims=True)
    parts = [part.astype(F32) for part in split3(half_norm)]
    row = lax.broadcasted_iota(jnp.int32, (16, width), 0)
    first = 3 if mine else 0
    extra = jnp.where(row < 6, 1.0, 0.0).astype(F32)
    for at, part in enumerate(parts):
        extra = jnp.where(row == first + at, part, extra)
    extra = extra.astype(BF16)
    order = [high, high, mid, high, low, mid] if mine else [high, mid, high, low, high, mid]
    used = 6 * points.shape[0] + 16
    total = -(-used // 256) * 256
    return jnp.concatenate(order + [extra, jnp.zeros((total - used, width), BF16)], axis=0)


def to_column(row, count, first):
    shape = (count, row.shape[1])
    same = lax.broadcasted_iota(jnp.int32, shape, 0) + first == lax.broadcasted_iota(jnp.int32, shape, 1)
    return jnp.sum(jnp.where(same, row, 0.0), axis=1, keepdims=True)


def to_row(column, width):
    shape = (column.shape[0], width)
    same = lax.broadcasted_iota(jnp.int32, shape, 0) == lax.broadcasted_iota(jnp.int32, shape, 1)
    return jnp.sum(jnp.where(same, column, 0.0), axis=0, keepdims=True)


def kernel(
    nblk, ncol,
    enc_hbm, w1_hbm, w2_hbm, inv_hbm, rhs_hbm,
    norm_ref, curve_ref, image_ref,
    enc, w1, w2_ref, inv_ref, xall, vall, rall, mine_t, acc, images, parts, sums,
    load_sem, x_recv, v_recv, r_recv, i_recv, s_recv,
    x_out_s, x_mid_s, x_col_s, x_core_s, v_out_s, v_mid_s, v_core_s, r_send, i_send, s_send,
):
    no = nblk // 4
    everyone = nblk * ncol
    blk = lax.axis_index("blk")
    col = lax.axis_index("col")
    out, mid, core = blk // 4, (blk // 2) % 2, blk % 2
    me = blk * ncol + col
    width = xall.shape[2]
    count = rall.shape[1]
    steps = 2 * no

    def blk_of(o, m, c):
        return (o * 2 + m) * 2 + c

    mid_peer = (blk_of(out, 1 - mid, core), col)
    core_peer = (blk_of(out, mid, 1 - core), col)

    def col_of(d):
        return lax.rem(col + d, ncol)

    def out_of(d):
        return blk_of(lax.rem(out + d, no), mid, core)

    def any_of(d):
        other = lax.rem(me + d, everyone)
        return other, (other // ncol, lax.rem(other, ncol))

    barrier = pltpu.get_barrier_semaphore()
    for d in range(1, everyone):
        pl.semaphore_signal(barrier, inc=1, device_id=any_of(d)[1], device_id_type=MESH)

    def half(k):
        return pl.ds(pl.multiple_of(k * width, width), width)

    my_rows = pl.ds(pl.multiple_of(col * count, count), count)
    loads = [
        pltpu.make_async_copy(source, target, load_sem.at[at])
        for at, (source, target) in enumerate(
            (
                (rhs_hbm, rall.at[col]),
                (rhs_hbm.at[:, half(col)], vall.at[blk, my_rows]),
                (enc_hbm, enc),
                (w1_hbm, w1),
                (w2_hbm, w2_ref),
                (inv_hbm, inv_ref),
            )
        )
    ]
    for load in loads:
        load.start()

    def remote(source, target, peer, send_sem, recv_sem):
        return pltpu.make_async_remote_copy(
            src_ref=source, dst_ref=target, send_sem=send_sem, recv_sem=recv_sem,
            device_id=peer, device_id_type=MESH,
        )

    def x_send(b, peer, sem):
        return remote(xall.at[b], xall.at[b], peer, sem, x_recv.at[b])

    def x_col_send(d):
        return remote(xall.at[blk], xall.at[nblk + col], (blk, col_of(d)), x_col_s.at[d], x_recv.at[nblk + col])

    def v_send(b, peer, sem):
        return remote(vall.at[b], vall.at[b], peer, sem, v_recv.at[b])

    def v_part(do, dk):
        k = col_of(dk)
        return remote(
            rall.at[col, :, half(k)], vall.at[blk, my_rows], (out_of(do), k), v_out_s.at[do, dk], v_recv.at[blk]
        )

    def r_copy(d):
        return remote(rall.at[col], rall.at[col], (blk, col_of(d)), r_send.at[d], r_recv.at[col])

    pieces = [(do, dk) for do in range(no) for dk in range(ncol) if do or dk]
    loads[0].wait()
    loads[1].wait()
    pl.semaphore_wait(barrier, everyone - 1)
    for do, dk in pieces:
        v_part(do, dk).start()

    for load in loads[2:]:
        load.wait()
    hidden = jnp.maximum(jnp.dot(enc[...], w1[...], preferred_element_type=F32), 0.0).astype(BF16)
    features = lax.dot_general(w2_ref[...], hidden, (((1,), (1,)), ((), ())), preferred_element_type=F32)
    xall[blk] = features * to_column(inv_ref[...], features.shape[0], 0)
    acc[...] = jnp.zeros_like(acc)

    for d in range(1, no):
        x_send(blk, (out_of(d), col), x_out_s.at[d]).start()
    x_send(blk, mid_peer, x_mid_s.at[0]).start()
    for d in range(1, ncol):
        x_col_send(d).start()
    x_send(blk, core_peer, x_core_s.at[0]).start()
    for d in range(1, ncol):
        r_copy(d).start()

    for dk in range(1, ncol):
        remote(
            vall.at[blk, my_rows], vall.at[blk, my_rows], core_peer, v_core_s.at[0], v_recv.at[blk]
        ).wait_recv()
    v_send(blk, mid_peer, v_mid_s.at[0]).start()
    v_send(blk, core_peer, v_core_s.at[0]).start()
    for d in range(1, no):
        b = out_of(d)
        v_send(b, mid_peer, v_mid_s.at[d]).wait_recv()
        v_send(b, mid_peer, v_mid_s.at[d]).start()
        v_send(b, core_peer, v_core_s.at[d]).start()

    mine_t[half(col), :] = stacked(xall[blk], True).T
    for d in range(1, ncol):
        k = col_of(d)
        x_send(nblk + k, core_peer, x_core_s.at[0]).wait_recv()
        mine_t[half(k), :] = stacked(xall[nblk + k], True).T

    def place(s):
        dm, do = s // no, s % no
        return lax.rem(out + do, no), lax.rem(mid + dm, 2)

    def product(b):
        rows = stacked(xall[b], False)
        vec = jnp.concatenate(split3(vall[b]), axis=0)
        logs = jnp.dot(mine_t[...], rows, preferred_element_type=F32)
        tile = jnp.exp2(logs).astype(BF16)
        return lax.dot_general(tile, vec, (((1,), (1,)), ((), ())), preferred_element_type=F32)

    def step(s, carry):
        @pl.when(jnp.logical_and(s < steps, s > 0))
        def _():
            o, m = place(s)
            b = blk_of(o, m, core)
            x_send(b, core_peer, x_core_s.at[s]).wait_recv()

            @pl.when(s < no)
            def _():
                x_send(b, mid_peer, x_mid_s.at[s]).start()

            x_send(b, core_peer, x_core_s.at[s]).start()

            @pl.when(s >= no)
            def _():
                v_send(b, core_peer, v_core_s.at[s]).wait_recv()
                v_send(b, core_peer, v_core_s.at[s]).start()

        @pl.when(s >= 2)
        def _():
            o, m = place(s - 2)
            other = blk_of(o, m, 1 - core)
            x_send(other, core_peer, x_core_s.at[s - 2]).wait_recv()
            v_send(other, core_peer, v_core_s.at[s - 2]).wait_recv()
            acc[...] += product(blk_of(o, m, core)) + product(other)

        return carry

    lax.fori_loop(0, steps + 2, step, 0)

    total = count * ncol
    acc_t = acc[...].T
    image = acc_t[:total] + acc_t[total : 2 * total] + acc_t[2 * total :]
    for k in range(ncol):
        images[k] = image[k * count : (k + 1) * count]

    def i_copy(d):
        return remote(images.at[col_of(d)], parts.at[col], (blk, col_of(d)), i_send.at[d], i_recv.at[col])

    def s_copy(d, at):
        return remote(sums.at[at], sums.at[at], any_of(d)[1], s_send.at[d], s_recv.at[at])

    for d in range(1, ncol):
        k = col_of(d)
        remote(rall.at[k], rall.at[k], (blk, k), r_send.at[d], r_recv.at[k]).wait_recv()
    bent = jnp.concatenate(
        [jnp.sum(rall[k] * image[k * count : (k + 1) * count], axis=1, keepdims=True) for k in range(ncol)], axis=0
    )
    norm = jnp.sum(vall[blk] * vall[blk], axis=1, keepdims=True)
    sums[me] = jnp.concatenate([to_row(bent, sums.shape[2]), to_row(norm, sums.shape[2])], axis=0)
    for d in range(1, everyone):
        s_copy(d, me).start()
    for d in range(1, ncol):
        i_copy(d).start()

    final = images[col]
    for d in range(1, ncol):
        k = col_of(d)
        remote(images.at[k], parts.at[k], (blk, k), i_send.at[d], i_recv.at[k]).wait_recv()
        final = final + parts[k]
    image_ref[...] = final
    for d in range(1, everyone):
        s_copy(d, any_of(d)[0]).wait_recv()
    whole = jnp.sum(sums[...], axis=0)
    curve_ref[...] = jnp.broadcast_to(to_column(whole[:1], count, col * count), final.shape)
    norm_ref[...] = jnp.broadcast_to(to_column(whole[1:], count, col * count), final.shape)

    for d in range(1, everyone):
        s_copy(d, me).wait_send()
    for d in range(1, ncol):
        i_copy(d).wait_send()
        r_copy(d).wait_send()
        x_col_send(d).wait_send()
    for do, dk in pieces:
        v_part(do, dk).wait_send()
    for d in range(1, no):
        x_send(blk, (out_of(d), col), x_out_s.at[d]).wait_send()

    def settle(s, carry):
        x_send(blk, core_peer, x_core_s.at[s]).wait_send()
        v_send(blk, core_peer, v_core_s.at[s]).wait_send()

        @pl.when(s < no)
        def _():
            x_send(blk, mid_peer, x_mid_s.at[s]).wait_send()
            v_send(blk, mid_peer, v_mid_s.at[s]).wait_send()

        return carry

    lax.fori_loop(0, steps, settle, 0)


def solution(mesh):
    nblk, ncol = mesh.shape["blk"], mesh.shape["col"]
    no = nblk // 4

    def on_device(encodings, first_weight, second_weight, inv_scale, outputscale, noise, rhs):
        half, feat = encodings.shape[0], second_weight.shape[1]
        cols, points = rhs.shape
        depth = -(-(6 * feat + 16) // 256) * 256
        dma = pltpu.SemaphoreType.DMA
        vmem = pl.BlockSpec(memory_space=pltpu.VMEM)
        hbm = pl.BlockSpec(memory_space=pl.ANY)
        out = jax.ShapeDtypeStruct(rhs.shape, F32)
        norm, curve, image = pl.pallas_call(
            functools.partial(kernel, nblk, ncol),
            out_shape=(out, out, out),
            in_specs=[hbm] * 5,
            out_specs=(vmem, vmem, vmem),
            scratch_shapes=[
                pltpu.VMEM(encodings.shape, BF16),
                pltpu.VMEM(first_weight.shape, BF16),
                pltpu.VMEM((feat, second_weight.shape[0]), BF16),
                pltpu.VMEM((1, feat), F32),
                pltpu.VMEM((nblk + ncol, feat, half), F32),
                pltpu.VMEM((nblk, ncol * cols, half), F32),
                pltpu.VMEM((ncol, cols, points), F32),
                pltpu.VMEM((points, depth), BF16),
                pltpu.VMEM((points, 3 * ncol * cols), F32),
                pltpu.VMEM((ncol, cols, points), F32),
                pltpu.VMEM((ncol, cols, points), F32),
                pltpu.VMEM((nblk * ncol, 2, 128), F32),
                dma((6,)),
                dma((nblk + ncol,)),
                dma((nblk,)),
                dma((ncol,)),
                dma((ncol,)),
                dma((nblk * ncol,)),
                dma((no,)),
                dma((no,)),
                dma((ncol,)),
                dma((2 * no,)),
                dma((no, ncol)),
                dma((no,)),
                dma((2 * no,)),
                dma((ncol,)),
                dma((ncol,)),
                dma((nblk * ncol,)),
            ],
            compiler_params=pltpu.CompilerParams(collective_id=0, has_side_effects=True),
        )(encodings, first_weight, second_weight.T, inv_scale.reshape(1, feat), rhs)
        alpha = norm / (outputscale * curve + noise * norm)
        return alpha * rhs, rhs - alpha * (outputscale * image + noise * rhs)

    placed = (P(("blk", "col"), None), P(), P(), P(), P(), P(), P("col", "blk"))
    return jax.shard_map(
        on_device,
        mesh=mesh,
        in_specs=placed,
        out_specs=(P("col", "blk"), P("col", "blk")),
        check_vma=False,
    )
```

time: 33.1 us -> 30.6 us (0.924)
  Pallas kernels: 29.5 us -> 27 us
    pallas_call x1, Pallas kernels: 29.5 us -> 27 us  [on_device(): pl.pallas_call(functools.partial(kernel, nblk, ncol), out_shape=(out, out...]
where the time goes in v3:
time: 30.6 us; the launch traced here: 30.4 us
  Pallas kernels  27 us (88%)
  between operations  1.95 us (6%)
  other arithmetic  1.44 us (5%)
    pallas_call x1, Pallas kernels, on_device(): pl.pallas_call(functools.partial(kernel, nblk, ncol), out_shape=(out, out...  27 us
    sub x1, other arithmetic, on_device(): return (alpha * rhs, rhs - alpha * (outputscale * image + noise * rhs))  1.44 us

profile of v3, /device:TPU:0, one launch (start us, length us, event | category | flops | bytes accessed | tf_op | source)
XLA Modules:
  0.0 30.4 jit_solution(10962047679755104419)
XLA Ops:
  1.9 0.0 copy-start
  1.9 27.0 %shard_map.86 = (f32[16,512]{1,0:T(8,128)}, f32[16,512]{1,0:T(8,128)}, f32[16,512]{1,0:T(8,128)}) custom-call(bf16[256,1024]{1,0:T(8,128)(2,1)} %enc_hbm.1, bf16[1024,512]{1,0:T(8,128)(2,1)} %w1_hbm.1, bf16[32,512]{1,0:T(8,128)(2,1)} %bitcast.6, f32[1,32]{1,0:T(1,128)} %bitcast.7, f32[16,512]{1,0:T(8,128)} %rhs_hbm.1), custom_call_target="tpu_custom_call" | custom-call | tf_op jit(solution)/shard_map/pallas_call | solution.py:293
  29.0 0.0 copy-done
  29.0 1.4 %multiply_subtract_fusion = (f32[16,512]{1,0:T(8,128)}, f32[16,512]{1,0:T(8,128)}) fusion(f32[16,512]{1,0:T(8,128)S(1)} %copy-done, f32[16,512]{1,0:T(8,128)} %get-tuple-element.7, f32[]{:T(128)} %bitcast.5, f32[]{:T(128)} %bitcast.4, f32[16,512]{1,0:T(8,128)} %get-tuple-element.5, f32[16,512]{1,0:T(8,128)} %get-tuple-element.6), kind=kLoop, calls=%fused_computation | loop fusion | flops 81920 | bytes 196616 | tf_op jit(solution)/shard_map/sub | solution.py:331
Async XLA Ops:
  1.9 27.0 %copy-start = (f32[16,512]{1,0:T(8,128)S(1)}, f32[16,512]{1,0:T(8,128)}, u32[]{:S(2)}) copy-start(f32[16,512]{1,0:T(8,128)} %rhs_hbm.1) | copy-start | bytes 98308
